TPU v7x, 32 devices: a whole 2x2x4 slice. The times are simulated.
32 devices in a mesh: front: 4 (over z), tile: 8 (over y, x, core).
Axes of the slice: x: 2, y: 2, z: 4, core: 2. Of those that a mesh axis runs over, the one named last changes fastest.
Arguments:
- lower_basis: bfloat16 [4, 8, 512, 1024], P('front', 'tile'), may hold values from -0.75 to 0.75
- lower_coeff: bfloat16 [4, 8, 512, 1024], P('front', 'tile'), may hold values from -0.75 to 0.75
- upper_basis: bfloat16 [4, 8, 512, 1024], P('front', 'tile'), may hold values from -0.75 to 0.75
- upper_coeff: bfloat16 [4, 8, 512, 1024], P('front', 'tile'), may hold values from -0.75 to 0.75
- lower_rank: int32 [4, 8, 32], P('front', 'tile'), may hold values from 1 to 32
- upper_rank: int32 [4, 8, 32], P('front', 'tile'), may hold values from 1 to 32
- child_half: int32 [4, 8], replicated, may hold values from 0 to 1
- owner_shift: int32 [1, 16], replicated, may hold values from 0 to 3
Outputs:
- parent_tiles: bfloat16 [4, 8, 4096, 512], P('front', 'tile')
Inputs may be any that keep to these rules, and one draw needn't show every extreme that they name: `child_half`: 0 keeps a tile's index, 1 moves it by 8.
All inputs are finite; a program needn't handle non-finite values.
Results may differ from a plain program's by a relative error of at most 0.0062.
Values may be sent and summed in bfloat16 or wider, within the bound.
A program may use at most 192 MiB of HBM per device.

v0:
```python
import functools

import jax
import jax.numpy as jnp
from jax import lax
from jax.experimental import pallas as pl
from jax.experimental.pallas import tpu as pltpu
from jax.sharding import PartitionSpec as P

MESH = pl.DeviceIdType.MESH
R = 32
GROUP = 256
CHUNKS = 2
WINDOW = 2
BF16, F32 = jnp.bfloat16, jnp.float32


def expand_ranks(rank_ref, rows, columns):
    col = lax.broadcasted_iota(jnp.int32, (rows, columns), 1)
    panel, within = col // R, col % R
    rank = jnp.zeros((rows, columns), jnp.int32)
    for k in range(columns // R):
        rank = jnp.where(panel == k, rank_ref[0, 0, k], rank)
    return within < rank


def schur_kernel(
    n, xb, yb, pb, qb, lr, ur, half_ref, shift_ref, recv,
    xbuf, ybuf, pbuf, qbuf, ptbuf, mbuf, wbuf, tbuf, zbuf,
    load_sem, send_sem, recv_sem, zsend_sem, zrecv_sem,
):
    block, columns = xb.shape[2:]
    rows = block // CHUNKS
    na = n // 4
    groups = columns // GROUP
    front, me = lax.axis_index("front"), lax.axis_index("tile")
    parent, z = front // 4, lax.rem(front, 4)
    a, b, c = me // 4, lax.rem(me // 2, 2), lax.rem(me, 2)
    turn = lax.rem(a - c + na, na)
    sib = me + 1 - 2 * c
    across = me + 2 - 4 * b
    peers = [lax.rem(a - d + na, na) * 4 + b * 2 + c for d in range(1, na)]

    def tile_of(ai, bi, ci):
        return ai * 4 + bi * 2 + ci

    def loads():
        return [
            pltpu.make_async_copy(yb.at[0, 0], ybuf.at[me], load_sem.at[0]),
            pltpu.make_async_copy(xb.at[0, 0], xbuf.at[me], load_sem.at[1]),
            pltpu.make_async_copy(pb.at[0, 0], pbuf, load_sem.at[2]),
            pltpu.make_async_copy(qb.at[0, 0], qbuf, load_sem.at[3]),
        ]

    for copy in loads():
        copy.start()

    barrier = pltpu.get_barrier_semaphore()
    for t in [sib, across] + peers:
        pl.semaphore_signal(barrier, inc=1, device_id={"tile": t}, device_id_type=MESH)
    for d in range(1, 4):
        pl.semaphore_signal(
            barrier, inc=1, device_id={"front": parent * 4 + lax.rem(z + d, 4)},
            device_id_type=MESH,
        )
    pl.semaphore_wait(barrier, 2 + len(peers) + 3)

    def send(kind, is_x, item, ch, target, own=False):
        buf = xbuf if is_x else ybuf
        at = pl.ds(pl.multiple_of(ch * rows, rows), rows)
        src = yb.at[0, 0, at] if own and not is_x else buf.at[item, at]
        s = ch + (CHUNKS if is_x else 0)
        return pltpu.make_async_remote_copy(
            src_ref=src, dst_ref=buf.at[item, at],
            send_sem=send_sem.at[kind, item, s], recv_sem=recv_sem.at[item, s],
            device_id={"tile": target}, device_id_type=MESH,
        )

    def arrived(is_x, item, ch):
        send(0, is_x, item, ch, sib).wait_recv()

    def for_chunks(body):
        def step(ch, carry):
            body(ch)
            return carry
        lax.fori_loop(0, CHUNKS, step, 0)

    def own_copies(p, is_x, ch, do):
        @pl.when(turn == p)
        def _():
            do(send(1, is_x, me, ch, across, True))
        if p > 0:
            do(send(1 + p, is_x, me, ch, peers[p - 1], True))

    def start(copy):
        copy.start()

    def own_ahead(p, is_x, ch):
        @pl.when(ch < CHUNKS - WINDOW)
        def _():
            own_copies(p, is_x, ch + WINDOW, start)

        p_next = p + 1 if is_x else p
        if p_next < na:
            @pl.when(ch >= CHUNKS - WINDOW)
            def _():
                own_copies(p_next, not is_x, ch + WINDOW - CHUNKS, start)

    for ch in range(WINDOW):
        own_copies(0, False, ch, start)
    for_chunks(lambda ch: send(0, False, me, ch, sib, True).start())
    ycopy, xcopy, pcopy, qcopy = loads()
    xcopy.wait()
    keep = expand_ranks(lr, rows, columns)

    def mask_x(ch):
        at = pl.ds(pl.multiple_of(ch * rows, rows), rows)
        xbuf[me, at] = jnp.where(keep, xbuf[me, at].astype(F32), 0.0).astype(BF16)

    for_chunks(mask_x)
    for_chunks(lambda ch: send(0, True, me, ch, sib, True).start())
    pcopy.wait()
    for g in range(groups):
        at = slice(g * GROUP, (g + 1) * GROUP)
        ptbuf[at, :] = jnp.transpose(pbuf[:, at].astype(F32)).astype(BF16)
    qcopy.wait()
    keep_q = expand_ranks(ur, rows, columns)

    def mask_q(ch):
        at = pl.ds(pl.multiple_of(ch * rows, rows), rows)
        qbuf[at] = jnp.where(keep_q, qbuf[at].astype(F32), 0.0).astype(BF16)

    for_chunks(mask_q)
    ycopy.wait()
    col_half = half_ref[front, me]
    shift = shift_ref[parent, me + n * col_half]

    def base(bi, ci):
        return jnp.where(bi == b, a, ci)

    def zsend(p, d, ch):
        at = pl.ds(pl.multiple_of(ch * rows, rows), rows)
        if d == 0:
            return pltpu.make_async_copy(
                zbuf.at[p, 0, at], recv.at[z, p, at], zsend_sem.at[p, 0, ch]
            )
        return pltpu.make_async_remote_copy(
            src_ref=zbuf.at[p, d, at], dst_ref=recv.at[z, p, at],
            send_sem=zsend_sem.at[p, d, ch], recv_sem=zrecv_sem.at[p, z, ch],
            device_id={"front": parent * 4 + lax.rem(z + d, 4)}, device_id_type=MESH,
        )

    def zarrived(p, d, ch):
        at = pl.ds(pl.multiple_of(ch * rows, rows), rows)
        source = lax.rem(z + d, 4)
        pltpu.make_async_remote_copy(
            src_ref=zbuf.at[p, d, at], dst_ref=recv.at[source, p, at],
            send_sem=zsend_sem.at[p, d, ch], recv_sem=zrecv_sem.at[p, source, ch],
            device_id={"front": parent * 4 + source}, device_id_type=MESH,
        ).wait_recv()

    def relays(p, do):
        near = tile_of(lax.rem(a + p, na), b, c)
        far_a = lax.rem(c + p, na)
        far = tile_of(far_a, 1 - b, c)

        def run(is_x, ch, wait=None):
            if p > 0:
                if wait:
                    wait(is_x, near, ch)
                if na == 2:
                    @pl.when(lax.rem(a + p, 2) != c)
                    def _():
                        do(1, is_x, near, ch, across)
                do(0, is_x, near, ch, sib)
            if wait:
                wait(is_x, far, ch)

            if na > 2 or p == 0:
                @pl.when(far_a == a)
                def _():
                    for d, t in enumerate(peers):
                        do(2 + d, is_x, far, ch, t)
            do(0, is_x, far, ch, sib)

        return run

    def do_start(kind, is_x, item, ch, target):
        send(kind, is_x, item, ch, target).start()

    def do_wait(kind, is_x, item, ch, target):
        send(kind, is_x, item, ch, target).wait_send()

    row = lax.broadcasted_iota(jnp.int32, (GROUP, GROUP), 0) // R
    col = lax.broadcasted_iota(jnp.int32, (GROUP, GROUP), 1) // R
    diagonal = row == col

    for p in range(na):
        forward = relays(p, do_start)
        items = [
            tile_of(lax.rem(base(rr // 2, rr % 2) + p, na), rr // 2, rr % 2)
            for rr in range(4)
        ]
        sib_near = tile_of(lax.rem(a + p, na), b, 1 - c)
        sib_far = tile_of(lax.rem(1 - c + p, na), 1 - b, 1 - c)

        def take(is_x, ch):
            forward(is_x, ch, arrived)
            own_ahead(p, is_x, ch)

        for_chunks(lambda ch: take(False, ch))

        def sib_y(ch):
            arrived(False, sib_near, ch)
            arrived(False, sib_far, ch)

        for_chunks(sib_y)
        for rr in range(4):
            for g in range(groups):
                at = slice(g * GROUP, (g + 1) * GROUP)
                middle = jnp.dot(
                    ptbuf[at, :], ybuf[items[rr], :, at], preferred_element_type=F32
                )
                mbuf[rr, g] = jnp.where(diagonal, middle, 0.0).astype(BF16)

        def step(ch):
            take(True, ch)
            arrived(True, sib_near, ch)
            arrived(True, sib_far, ch)
            at = pl.ds(pl.multiple_of(ch * rows, rows), rows)
            for rr in range(4):
                for g in range(groups):
                    cols = slice(g * GROUP, (g + 1) * GROUP)
                    wbuf[rr * rows:(rr + 1) * rows, cols] = lax.dot_general(
                        xbuf[items[rr], at, cols], mbuf[rr, g],
                        (((1,), (1,)), ((), ())), preferred_element_type=F32,
                    ).astype(BF16)
            for rr in range(4):
                tbuf[rr] = lax.dot_general(
                    wbuf[rr * rows:(rr + 1) * rows, :], qbuf[...],
                    (((1,), (1,)), ((), ())), preferred_element_type=F32,
                ).astype(BF16)
            for d in range(4):
                residue = lax.rem(z + d - shift + 4, 4)
                zbuf[p, d, at] = tbuf[residue]
            for d in (2, 3, 1, 0):
                zsend(p, d, ch).start()

        for_chunks(step)

    def drain(ch):
        for is_x in (False, True):
            send(0, is_x, me, ch, sib, True).wait_send()
            for p in range(na):
                own_copies(p, is_x, ch, lambda copy: copy.wait_send())
            for p in range(na):
                relays(p, do_wait)(is_x, ch)

    for_chunks(drain)

    def zdrain(ch):
        for p in range(na):
            zsend(p, 0, ch).wait()
            for d in range(1, 4):
                zsend(p, d, ch).wait_send()
            for d in range(1, 4):
                zarrived(p, d, ch)

    for_chunks(zdrain)


def assemble_kernel(n, half_ref, shift_ref, recv, out):
    na = n // 4
    front, me = lax.axis_index("front"), lax.axis_index("tile")
    parent, z = front // 4, lax.rem(front, 4)
    a, b = me // 4, lax.rem(me // 2, 2)
    source = []
    for s in range(4):
        child = 4 * parent + s
        col_half = half_ref[child, me]
        residue = lax.rem(z - shift_ref[parent, me + n * col_half] + 4, 4)
        start = jnp.where(residue // 2 == b, a, lax.rem(residue, 2))
        source.append((child, col_half, residue, start))
    for q in range(na):
        picked = []
        for s, (child, col_half, residue, start) in enumerate(source):
            p = lax.rem(q - start + na, na)
            picked.append((recv[s, p], col_half * 2 + half_ref[child, 4 * q + residue]))
        for halves in range(4):
            total = jnp.zeros(out.shape[1:], F32)
            for tile, own in picked:
                total = total + jnp.where(own == halves, tile.astype(F32), 0.0)
            slot = (halves // 2) * (n // 2) + (halves % 2) * na + q
            out[slot] = total.astype(out.dtype)


def solution(mesh):
    n = mesh.shape["tile"]
    na = n // 4

    def per_device(xb, yb, pb, qb, lr, ur, half, shift):
        block, columns = xb.shape[2:]
        rows = block // CHUNKS
        anywhere = pl.BlockSpec(memory_space=pl.ANY)
        scalars = pl.BlockSpec(memory_space=pltpu.SMEM)
        received = pl.pallas_call(
            functools.partial(schur_kernel, n),
            out_shape=jax.ShapeDtypeStruct((4, na, block, block), BF16),
            in_specs=[anywhere] * 4 + [scalars] * 4,
            out_specs=anywhere,
            scratch_shapes=[
                pltpu.VMEM((n, block, columns), BF16),
                pltpu.VMEM((n, block, columns), BF16),
                pltpu.VMEM((block, columns), BF16),
                pltpu.VMEM((block, columns), BF16),
                pltpu.VMEM((columns, block), BF16),
                pltpu.VMEM((4, columns // GROUP, GROUP, GROUP), BF16),
                pltpu.VMEM((4 * rows, columns), BF16),
                pltpu.VMEM((4, rows, block), BF16),
                pltpu.VMEM((na, 4, block, block), BF16),
                pltpu.SemaphoreType.DMA((4,)),
                pltpu.SemaphoreType.DMA((na + 1, n, 2 * CHUNKS)),
                pltpu.SemaphoreType.DMA((n, 2 * CHUNKS)),
                pltpu.SemaphoreType.DMA((na, 4, CHUNKS)),
                pltpu.SemaphoreType.DMA((na, 4, CHUNKS)),
            ],
            compiler_params=pltpu.CompilerParams(
                collective_id=0, has_side_effects=True, vmem_limit_bytes=60 * 2**20
            ),
        )(xb, yb, pb, qb, lr, ur, half, shift)
        strip = 128
        out = pl.pallas_call(
            functools.partial(assemble_kernel, n),
            grid=(block // strip,),
            out_shape=jax.ShapeDtypeStruct((n, block, block), BF16),
            in_specs=[scalars, scalars,
                      pl.BlockSpec((4, na, strip, block), lambda r: (0, 0, r, 0))],
            out_specs=pl.BlockSpec((n, strip, block), lambda r: (0, r, 0)),
        )(half, shift, received)
        return out.reshape(1, 1, n * block, block)

    split = P("front", "tile", None, None)
    ranks = P("front", "tile", None)
    return jax.shard_map(
        per_device, mesh=mesh,
        in_specs=(split, split, split, split, ranks, ranks, P(), P()),
        out_specs=split, check_vma=False,
    )
```

profile of v0, /device:TPU:9, one launch (start us, length us, event | category | flops | bytes accessed | tf_op | source)
XLA Modules:
  0.0 149.9 jit_solution(17763989189278777011)
XLA Ops:
  0.0 143.9 %shard_map.82.recv = bf16[4,2,512,512]{3,2,1,0:T(8,128)(2,1)} custom-call(bf16[1,1,512,1024]{3,2,1,0:T(8,128)(2,1)} %xb.1, bf16[1,1,512,1024]{3,2,1,0:T(8,128)(2,1)} %yb.1, bf16[1,1,512,1024]{3,2,1,0:T(8,128)(2,1)} %pb.1, bf16[1,1,512,1024]{3,2,1,0:T(8,128)(2,1)} %qb.1, s32[1,1,32]{2,1,0:T(1,128)} %lr.1, s32[1,1,32]{2,1,0:T(1,128)} %ur.1, s32[4,8]{1,0:T(4,128)} %half_ref.3, ...), custom_call_target="tpu_custom_call" | custom-call | tf_op jit(solution)/shard_map/pallas_call | solution.py:306
  143.9 6.0 %shard_map.83 = bf16[8,512,512]{2,1,0:T(8,128)(2,1)} custom-call(s32[4,8]{1,0:T(4,128)} %half_ref.3, s32[1,16]{1,0:T(1,128)} %shift_ref.3, bf16[4,2,512,512]{3,2,1,0:T(8,128)(2,1)} %shard_map.82.recv), custom_call_target="tpu_custom_call" | custom-call | tf_op jit(solution)/shard_map/pallas_call | solution.py:332
where the time goes:
time: 150 us
  Pallas kernels  150 us (100%)
    pallas_call x1, Pallas kernels, per_device(): pl.pallas_call(functools.partial(schur_kernel, n), out_shape=jax.ShapeDty...  144 us
    pallas_call x1, Pallas kernels, per_device(): pl.pallas_call(functools.partial(assemble_kernel, n), grid=(block // stri...  5.96 us

commit v1 on v0

v1 whole, which is shorter than its diff:
```python
import functools

import jax
import jax.numpy as jnp
from jax import lax
from jax.experimental import pallas as pl
from jax.experimental.pallas import tpu as pltpu
from jax.sharding import PartitionSpec as P

MESH = pl.DeviceIdType.MESH
R = 32
YC = 8
XC = 8
LAG = 2
AHEAD = 3
STRIP = 16
LANES = 256
VMEM_OUT = 6 * 2**20
BF16, F32 = jnp.bfloat16, jnp.float32


def rank_mask(rank_ref, columns):
    col = lax.broadcasted_iota(jnp.int32, (8, columns), 1)
    panel, within = col // R, col % R
    rank = jnp.zeros((8, columns), jnp.int32)
    for k in range(columns // R):
        rank = jnp.where(panel == k, rank_ref[0, 0, k], rank)
    return jnp.where(within < rank, 1.0, 0.0).astype(F32)


def schur_kernel(
    n, staged, xb, yb, pb, qb, lr, ur, half_ref, shift_ref, out,
    xbuf, ybuf, pbuf, qbuf, ptbuf, qtbuf, nbuf, tbuf, zbuf, recv, keep_q, obuf,
    load_sem, send_sem, recv_sem, zsend_sem, zrecv_sem, out_sem,
):
    block, columns = xb.shape[2:]
    rows, group = block // XC, columns // YC
    na = n // 4
    front, me = lax.axis_index("front"), lax.axis_index("tile")
    parent, z = front // 4, lax.rem(front, 4)
    a, b, c = me // 4, lax.rem(me // 2, 2), lax.rem(me, 2)
    turn = lax.rem(a - c + na, na)
    sib = me + 1 - 2 * c
    across = me + 2 - 4 * b
    peers = [lax.rem(a - d + na, na) * 4 + b * 2 + c for d in range(1, na)]

    def tile_of(ai, bi, ci):
        return ai * 4 + bi * 2 + ci

    def rows_at(ch):
        return pl.ds(pl.multiple_of(ch * rows, rows), rows)

    def cols_at(j):
        return pl.ds(pl.multiple_of(j * group, group), group)

    def loads():
        return [
            pltpu.make_async_copy(xb.at[0, 0], xbuf.at[me], load_sem.at[0]),
            pltpu.make_async_copy(yb.at[0, 0], ybuf.at[me], load_sem.at[1]),
            pltpu.make_async_copy(pb.at[0, 0], pbuf, load_sem.at[2]),
            pltpu.make_async_copy(qb.at[0, 0], qbuf, load_sem.at[3]),
        ]

    for copy in loads():
        copy.start()

    barrier = pltpu.get_barrier_semaphore()
    for t in [sib, across] + peers:
        pl.semaphore_signal(barrier, inc=1, device_id={"tile": t}, device_id_type=MESH)
    for d in range(1, 4):
        pl.semaphore_signal(
            barrier, inc=1, device_id={"front": parent * 4 + lax.rem(z + d, 4)},
            device_id_type=MESH,
        )
    pl.semaphore_wait(barrier, 2 + len(peers) + 3)

    def send(kind, is_x, item, ch, target, own=False):
        if is_x:
            src = dst = xbuf.at[item, rows_at(ch)]
            s = ch + YC
        else:
            dst = ybuf.at[item, :, cols_at(ch)]
            src = yb.at[0, 0, :, cols_at(ch)] if own else dst
            s = ch
        return pltpu.make_async_remote_copy(
            src_ref=src, dst_ref=dst,
            send_sem=send_sem.at[kind, item, s], recv_sem=recv_sem.at[item, s],
            device_id={"tile": target}, device_id_type=MESH,
        )

    def arrived(is_x, item, ch):
        send(0, is_x, item, ch, sib).wait_recv()

    def loop(count, body):
        def step(i, carry):
            body(i)
            return carry
        lax.fori_loop(0, count, step, 0)

    def chunks(is_x):
        return XC if is_x else YC

    def own_copies(p, is_x, ch, do):
        @pl.when(turn == p)
        def _():
            do(send(1, is_x, me, ch, across, True))
        if p > 0:
            do(send(1 + p, is_x, me, ch, peers[p - 1], True))

    def start(copy):
        copy.start()

    def own_start(p, is_x):
        loop(chunks(is_x), lambda ch: own_copies(p, is_x, ch, start))

    def open_y(j):
        own_copies(0, False, j, start)
        send(0, False, me, j, sib, True).start()

    loop(YC, open_y)
    xcopy, ycopy, pcopy, qcopy = loads()
    xcopy.wait()
    keep_x = rank_mask(lr, columns)[:1]

    def open_x(ch):
        at = rows_at(ch)
        xbuf[me, at] = (xbuf[me, at].astype(F32) * keep_x).astype(BF16)

    loop(XC, open_x)

    def open_x_send(ch):
        own_copies(0, True, ch, start)
        send(0, True, me, ch, sib, True).start()

    loop(XC, open_x_send)
    keep_q[...] = rank_mask(ur, columns)
    col_half = half_ref[front, me]
    shift = shift_ref[parent, me + n * col_half]

    def residue_of(d):
        return lax.rem(z + d - shift + 4, 4)

    second = 3 - 2 * lax.rem(z, 2)
    third = 4 - second

    def zsend(p, d, ch):
        at = rows_at(ch)
        return pltpu.make_async_remote_copy(
            src_ref=zbuf.at[p, d - 1, at], dst_ref=recv.at[z, p, at],
            send_sem=zsend_sem.at[p, d - 1, ch], recv_sem=zrecv_sem.at[p, z, ch],
            device_id={"front": parent * 4 + lax.rem(z + d, 4)}, device_id_type=MESH,
        )

    def zarrived(p, d, ch):
        at = rows_at(ch)
        source = lax.rem(z + d, 4)
        pltpu.make_async_remote_copy(
            src_ref=zbuf.at[p, d - 1, at], dst_ref=recv.at[source, p, at],
            send_sem=zsend_sem.at[p, d - 1, ch], recv_sem=zrecv_sem.at[p, source, ch],
            device_id={"front": parent * 4 + source}, device_id_type=MESH,
        ).wait_recv()

    def near_forward(p, is_x, ch, do, wait):
        near = tile_of(lax.rem(a + p, na), b, c)
        if wait:
            arrived(is_x, near, ch)
        if na == 2:
            @pl.when(lax.rem(a + p, 2) != c)
            def _():
                do(send(1, is_x, near, ch, across))
        do(send(0, is_x, near, ch, sib))

    def far_forward(p, is_x, ch, do, wait):
        far_a = lax.rem(c + p, na)
        far = tile_of(far_a, 1 - b, c)
        if wait:
            arrived(is_x, far, ch)
        if na > 2 or p == 0:
            @pl.when(far_a == a)
            def _():
                for d, t in enumerate(peers):
                    do(send(2 + d, is_x, far, ch, t))
        do(send(0, is_x, far, ch, sib))

    row = lax.broadcasted_iota(jnp.int32, (group, 2 * group), 0) // R
    col = lax.rem(lax.broadcasted_iota(jnp.int32, (group, 2 * group), 1), group) // R
    diagonal = row == col

    def prepare(j):
        at = cols_at(j)
        ptbuf[at, :] = jnp.transpose(pbuf[:, at].astype(F32)).astype(BF16)
        kept = qbuf[:, at].astype(F32) * keep_q[:1, at]
        qtbuf[at, :] = jnp.transpose(kept).astype(BF16)

    def middles(j, first, second_item, slot):
        at = cols_at(j)
        y = jnp.concatenate([ybuf[first, :, at], ybuf[second_item, :, at]], axis=1)
        middle = jnp.dot(ptbuf[at, :], y, preferred_element_type=F32)
        middle = jnp.transpose(jnp.where(diagonal, middle, 0.0)).astype(BF16)
        both = jnp.dot(middle, qtbuf[at, :], preferred_element_type=F32).astype(BF16)
        nbuf[slot, at, :] = both[:group]
        nbuf[slot + 1, at, :] = both[group:]

    for p in range(na):
        near = tile_of(lax.rem(a + p, na), b, c)
        sib_near = tile_of(lax.rem(a + p, na), b, 1 - c)
        far = tile_of(lax.rem(c + p, na), 1 - b, c)
        sib_far = tile_of(lax.rem(1 - c + p, na), 1 - b, 1 - c)
        lag = jnp.where(lax.rem(c + p, na) == a, LAG, 0)
        behind = 0 if p == 0 else 1

        def near_middles(j):
            arrived(False, sib_near, j)
            middles(j, near, sib_near, 0)

        def far_middles(j):
            arrived(False, sib_far, j)
            middles(j, far, sib_far, 2)

        def when_in(i, count, body):
            @pl.when((i >= 0) & (i < count))
            def _():
                body(i)

        if p == 0:
            ycopy.wait()
            pcopy.wait()
            qcopy.wait()

            def open_near(j):
                prepare(j)
                near_middles(j)

            loop(AHEAD, open_near)

        def y_step(j):
            if p > 0:
                when_in(j, YC, lambda i: near_forward(p, False, i, start, True))
            when_in(j - behind, YC, lambda i: far_forward(p, False, i, start, True))
            if p == 0:
                when_in(j + AHEAD, YC, open_near)
            else:
                when_in(j - behind - lag, YC, near_middles)
            when_in(j - behind - lag, YC, far_middles)

        loop(YC + behind + LAG, y_step)

        def process(ch):
            arrived(True, sib_near, ch)
            arrived(True, sib_far, ch)
            at = rows_at(ch)
            for slot, (item, bi, ci) in enumerate(
                [(near, b, c), (sib_near, b, 1 - c), (far, 1 - b, c), (sib_far, 1 - b, 1 - c)]
            ):
                tbuf[bi * 2 + ci] = jnp.dot(
                    xbuf[item, at, :], nbuf[slot], preferred_element_type=F32
                ).astype(BF16)
            for d in (2, second, third):
                zbuf[p, d - 1, at] = tbuf[residue_of(d)]
                zsend(p, d, ch).start()
            recv[z, p, at] = tbuf[residue_of(0)]

        def x_step(ch):
            if p > 0:
                when_in(ch, XC, lambda i: near_forward(p, True, i, start, True))
            when_in(ch - behind, XC, lambda i: far_forward(p, True, i, start, True))
            if p + 1 < na:
                @pl.when(ch == XC - 1 + behind)
                def _():
                    own_start(p + 1, False)
                    own_start(p + 1, True)
            when_in(ch - behind - lag, XC, process)

        loop(XC + behind + LAG, x_step)

    def drain(is_x, ch):
        def wait_send(copy):
            copy.wait_send()
        send(0, is_x, me, ch, sib, True).wait_send()
        for p in range(na):
            own_copies(p, is_x, ch, wait_send)
            if p > 0:
                near_forward(p, is_x, ch, wait_send, False)
            far_forward(p, is_x, ch, wait_send, False)

    loop(YC, lambda ch: drain(False, ch))
    loop(XC, lambda ch: drain(True, ch))

    source = []
    for s in range(4):
        child = 4 * parent + s
        half = half_ref[child, me]
        residue = lax.rem(z - shift_ref[parent, me + n * half] + 4, 4)
        begin = jnp.where(residue // 2 == b, a, lax.rem(residue, 2))
        source.append((
            [lax.rem(q - begin + na, na) for q in range(na)],
            [half * 2 + half_ref[child, 4 * q + residue] for q in range(na)],
        ))

    def assemble(ch):
        for p in range(na):
            for d in range(1, 4):
                zarrived(p, d, ch)

        def strip(i):
            at = pl.ds(pl.multiple_of(ch * rows + i * STRIP, STRIP), STRIP)
            to = pl.ds(pl.multiple_of(i * STRIP, STRIP), STRIP) if staged else at
            target = obuf if staged else out
            for k in range(block // LANES):
                lanes = slice(k * LANES, (k + 1) * LANES)
                held = [
                    [recv[s, p, at, lanes].astype(F32) for p in range(na)] for s in range(4)
                ]
                for q in range(na):
                    picked = []
                    for s, (order, owner) in enumerate(source):
                        tile = held[s][0]
                        for p in range(1, na):
                            tile = jnp.where(order[q] == p, held[s][p], tile)
                        picked.append((tile, owner[q]))
                    for halves in range(4):
                        total = None
                        for tile, own in picked:
                            term = jnp.where(own == halves, tile, 0.0)
                            total = term if total is None else total + term
                        slot = (halves // 2) * (n // 2) + (halves % 2) * na + q
                        target[slot, to, lanes] = total.astype(BF16)

        loop(rows // STRIP, strip)
        if staged:
            copy = pltpu.make_async_copy(obuf, out.at[:, rows_at(ch)], out_sem)
            copy.start()
            copy.wait()

    loop(XC, assemble)

    def zdrain(ch):
        for p in range(na):
            for d in range(1, 4):
                zsend(p, d, ch).wait_send()

    loop(XC, zdrain)


def solution(mesh):
    n = mesh.shape["tile"]
    na = n // 4

    def per_device(xb, yb, pb, qb, lr, ur, half, shift):
        block, columns = xb.shape[2:]
        rows = block // XC
        anywhere = pl.BlockSpec(memory_space=pl.ANY)
        scalars = pl.BlockSpec(memory_space=pltpu.SMEM)
        shape = (n, block, block)
        staged = 2 * n * block * block > VMEM_OUT
        out = pl.pallas_call(
            functools.partial(schur_kernel, n, staged),
            out_shape=jax.ShapeDtypeStruct(shape, BF16) if staged else pltpu.VMEM(shape, BF16),
            in_specs=[anywhere] * 4 + [scalars] * 4,
            out_specs=anywhere if staged else pl.BlockSpec(memory_space=pltpu.VMEM),
            scratch_shapes=[
                pltpu.VMEM((n, block, columns), BF16),
                pltpu.VMEM((n, block, columns), BF16),
                pltpu.VMEM((block, columns), BF16),
                pltpu.VMEM((block, columns), BF16),
                pltpu.VMEM((columns, block), BF16),
                pltpu.VMEM((columns, block), BF16),
                pltpu.VMEM((4, columns, block), BF16),
                pltpu.VMEM((4, rows, block), BF16),
                pltpu.VMEM((na, 3, block, block), BF16),
                pltpu.VMEM((4, na, block, block), BF16),
                pltpu.VMEM((8, columns), F32),
                pltpu.VMEM((n, rows, block) if staged else (1, STRIP, block), BF16),
                pltpu.SemaphoreType.DMA((4,)),
                pltpu.SemaphoreType.DMA((na + 1, n, YC + XC)),
                pltpu.SemaphoreType.DMA((n, YC + XC)),
                pltpu.SemaphoreType.DMA((na, 3, XC)),
                pltpu.SemaphoreType.DMA((na, 4, XC)),
                pltpu.SemaphoreType.DMA,
            ],
            compiler_params=pltpu.CompilerParams(
                collective_id=0, has_side_effects=True,
                vmem_limit_bytes=(63 if staged else 56) * 2**20,
            ),
        )(xb, yb, pb, qb, lr, ur, half, shift)
        return out.reshape(1, 1, n * block, block)

    split = P("front", "tile", None, None)
    ranks = P("front", "tile", None)
    return jax.shard_map(
        per_device, mesh=mesh,
        in_specs=(split, split, split, split, ranks, ranks, P(), P()),
        out_specs=split, check_vma=False,
    )
```

time: 150 us -> 136 us (0.907)
  the two profiles are of different devices: /device:TPU:9 before, /device:TPU:0 now
where the time goes in v1:
time: 136 us; the launch traced here: 135 us
  Pallas kernels  133 us (98%)
  local copies, waits for them, and re-layouts  2.02 us (1%)
    pallas_call x1, Pallas kernels, per_device(): pl.pallas_call(functools.partial(schur_kernel, n, staged), out_shape=jax....  133 us

profile of v1, /device:TPU:0, one launch (start us, length us, event | category | flops | bytes accessed | tf_op | source)
XLA Modules:
  0.0 135.5 jit_solution(2084632897987125172)
XLA Ops:
  0.0 133.5 %shard_map.82 = bf16[8,512,512]{2,1,0:T(8,128)(2,1)S(1)} custom-call(bf16[1,1,512,1024]{3,2,1,0:T(8,128)(2,1)} %xb.1, bf16[1,1,512,1024]{3,2,1,0:T(8,128)(2,1)} %yb.1, bf16[1,1,512,1024]{3,2,1,0:T(8,128)(2,1)} %pb.1, bf16[1,1,512,1024]{3,2,1,0:T(8,128)(2,1)} %qb.1, s32[1,1,32]{2,1,0:T(1,128)} %lr.1, s32[1,1,32]{2,1,0:T(1,128)} %ur.1, s32[4,8]{1,0:T(4,128)} %half_ref.1, ...), custom_call_target="tpu_custom_call" | custom-call | tf_op jit(solution)/shard_map/pallas_call | solution.py:356
  133.5 2.0 %copy.10 = bf16[1,1,4096,512]{3,2,1,0:T(8,128)(2,1)} copy(bf16[1,1,4096,512]{3,2,1,0:T(8,128)(2,1)S(1)} %bitcast.1) | data formatting | bytes 8388608

commit v2 on v1

v2 whole, which is shorter than its diff:
```python
import functools

import jax
import jax.numpy as jnp
from jax import lax
from jax.experimental import pallas as pl
from jax.experimental.pallas import tpu as pltpu
from jax.sharding import PartitionSpec as P

MESH = pl.DeviceIdType.MESH
R = 32
YC = (8, 4)
XC = (8, 4)
LAG = 3
AHEAD = 3
STRIP = 16
LANES = 256
SIB_NEAR, SIB_FAR, FAR, NEAR = range(4)
VMEM_OUT = 6 * 2**20
BF16, F32 = jnp.bfloat16, jnp.float32


def rank_mask(rank_ref, columns):
    col = lax.broadcasted_iota(jnp.int32, (8, columns), 1)
    panel, within = col // R, col % R
    rank = jnp.zeros((8, columns), jnp.int32)
    for k in range(columns // R):
        rank = jnp.where(panel == k, rank_ref[0, 0, k], rank)
    return jnp.where(within < rank, 1.0, 0.0).astype(F32)


def chunks(is_x, p):
    return (XC if is_x else YC)[min(p, 1)]


def schur_kernel(
    n, staged, xb, yb, pb, qb, lr_hbm, ur_hbm, half_hbm, shift_hbm, out,
    xbuf, ybuf, pbuf, qbuf, ptbuf, qtbuf, nbuf, xs, zbuf, recv, keep_q, obuf,
    lr, ur, half_ref, shift_ref,
    load_sem, send_sem, first_sem, recv_sem, zsend_sem, zearly_sem, zlast_sem, know_sem, out_sem,
):
    block, columns = xb.shape[2:]
    na = n // 4
    front, me = lax.axis_index("front"), lax.axis_index("tile")
    parent, z = front // 4, lax.rem(front, 4)
    a, b, c = me // 4, lax.rem(me // 2, 2), lax.rem(me, 2)
    turn = lax.rem(a - c + na, na)
    sib = me + 1 - 2 * c
    across = me + 2 - 4 * b
    peers = [lax.rem(a - d + na, na) * 4 + b * 2 + c for d in range(1, na)]

    def tile_of(ai, bi, ci):
        return ai * 4 + bi * 2 + ci

    def rows_at(p, ch):
        rows = block // chunks(True, p)
        return pl.ds(pl.multiple_of(ch * rows, rows), rows)

    def cols_at(p, j):
        group = columns // chunks(False, p)
        return pl.ds(pl.multiple_of(j * group, group), group)

    def loads():
        pairs = [
            (yb.at[0, 0], ybuf.at[me]), (xb.at[0, 0], xbuf.at[me]), (lr_hbm, lr),
            (pb.at[0, 0], pbuf), (qb.at[0, 0], qbuf), (ur_hbm, ur),
            (half_hbm, half_ref), (shift_hbm, shift_ref),
        ]
        return [
            pltpu.make_async_copy(src, dst, load_sem.at[i])
            for i, (src, dst) in enumerate(pairs)
        ]

    for copy in loads():
        copy.start()

    def greet(sem, axes):
        pl.semaphore_signal(sem, inc=1, device_id=axes, device_id_type=MESH)

    barrier = pltpu.get_barrier_semaphore()
    for t in [sib, across] + peers:
        greet(barrier, {"tile": t})

    @pl.when(z > 0)
    def _():
        greet(barrier, {"front": front - 1})

    @pl.when(z < 3)
    def _():
        greet(barrier, {"front": front + 1})

    ycopy, xcopy, lrcopy, pcopy, qcopy, urcopy, halfcopy, shiftcopy = loads()
    ycopy.wait()
    inner = (z > 0) & (z < 3)
    pl.semaphore_wait(barrier, 3 + len(peers) + jnp.where(inner, 1, 0))

    def send(p, kind, role, is_x, item, ch, target):
        if is_x:
            part = xbuf.at[item] if ch is None else xbuf.at[item, rows_at(p, ch)]
            s = 0 if ch is None else ch + YC[min(p, 1)]
        else:
            part = ybuf.at[item] if ch is None else ybuf.at[item, :, cols_at(p, ch)]
            s = 0 if ch is None else ch
        landed = first_sem.at[role, s] if p == 0 else recv_sem.at[p - 1, role, s]
        return pltpu.make_async_remote_copy(
            src_ref=part, dst_ref=part,
            send_sem=send_sem.at[p, kind, int(is_x)], recv_sem=landed,
            device_id={"tile": target}, device_id_type=MESH,
        )

    def arrived(p, role, is_x, item, ch):
        send(p, 0, role, is_x, item, ch, sib).wait_recv()

    def loop(count, body):
        def step(i, carry):
            body(i)
            return carry
        lax.fori_loop(0, count, step, 0)

    def own_copies(p, is_x, ch, do):
        @pl.when(turn == p)
        def _():
            do(send(p, 1, FAR, is_x, me, ch, across))
        if p > 0:
            do(send(p, 2, NEAR, is_x, me, ch, peers[p - 1]))
        else:
            do(send(p, 0, SIB_NEAR, is_x, me, ch, sib))

    def start(copy):
        copy.start()

    def own_start(p, is_x):
        loop(chunks(is_x, p), lambda ch: own_copies(p, is_x, ch, start))

    own_start(0, False)

    @pl.when(inner)
    def _():
        greet(know_sem.at[0], {"front": front - 1})
        greet(know_sem.at[1], {"front": front + 1})

    xcopy.wait()
    lrcopy.wait()
    keep_x = rank_mask(lr, columns)[:1]

    def open_x(ch):
        at = rows_at(0, ch)
        xbuf[me, at] = (xbuf[me, at].astype(F32) * keep_x).astype(BF16)

    loop(chunks(True, 0), open_x)
    own_start(0, True)
    urcopy.wait()
    halfcopy.wait()
    shiftcopy.wait()
    keep_q[...] = rank_mask(ur, columns)
    col_half = half_ref[front, me]
    shift = shift_ref[parent, me + n * col_half]

    def residue_of(d):
        return lax.rem(z + d - shift + 4, 4)

    second = 3 - 2 * lax.rem(z, 2)
    third = 4 - second

    def zcopy(p, d, ch, source, mine):
        at = rows_at(p, ch)
        landed = zlast_sem.at[mine, ch] if p == na - 1 else zearly_sem.at[mine]
        return pltpu.make_async_remote_copy(
            src_ref=zbuf.at[d - 1, p, at], dst_ref=recv.at[source, p, at],
            send_sem=zsend_sem.at[d - 1], recv_sem=landed,
            device_id={"front": parent * 4 + lax.rem(z + d, 4)}, device_id_type=MESH,
        )

    def whole(d, count, sends):
        ref = zbuf.at[d - 1] if sends else recv.at[lax.rem(z + d, 4), pl.ds(0, count)]
        other = zbuf.at[d - 1, pl.ds(0, count)]
        return pltpu.make_async_remote_copy(
            src_ref=ref if sends else other, dst_ref=ref if not sends else other,
            send_sem=zsend_sem.at[d - 1], recv_sem=zearly_sem.at[d - 1],
            device_id={"front": parent * 4 + lax.rem(z + d, 4)}, device_id_type=MESH,
        )

    def near_forward(p, is_x, ch, do, wait):
        near = tile_of(lax.rem(a + p, na), b, c)
        if wait:
            arrived(p, NEAR, is_x, near, ch)
        if na == 2:
            @pl.when(lax.rem(a + p, 2) != c)
            def _():
                do(send(p, 3, FAR, is_x, near, ch, across))
        do(send(p, 4, SIB_NEAR, is_x, near, ch, sib))

    def far_forward(p, is_x, ch, do, wait):
        far_a = lax.rem(c + p, na)
        far = tile_of(far_a, 1 - b, c)
        if wait:
            arrived(p, FAR, is_x, far, ch)
        if na > 2 or p == 0:
            @pl.when(far_a == a)
            def _():
                for d, t in enumerate(peers):
                    do(send(p, 6 + d, FAR, is_x, far, ch, t))
        do(send(p, 5, SIB_FAR, is_x, far, ch, sib))

    def prepare(j):
        at = cols_at(0, j)
        ptbuf[at, :] = jnp.transpose(pbuf[:, at].astype(F32)).astype(BF16)
        kept = qbuf[:, at].astype(F32) * keep_q[:1, at]
        qtbuf[at, :] = jnp.transpose(kept).astype(BF16)

    def middles(p, j, first, second_item, to_first, to_second):
        at = cols_at(p, j)
        group = columns // chunks(False, p)
        row = lax.broadcasted_iota(jnp.int32, (group, 2 * group), 0) // R
        col = lax.rem(lax.broadcasted_iota(jnp.int32, (group, 2 * group), 1), group) // R
        y = jnp.concatenate([ybuf[first, :, at], ybuf[second_item, :, at]], axis=1)
        middle = jnp.dot(ptbuf[at, :], y, preferred_element_type=F32)
        middle = jnp.transpose(jnp.where(row == col, middle, 0.0)).astype(BF16)
        both = jnp.dot(middle, qtbuf[at, :], preferred_element_type=F32).astype(BF16)
        nbuf[to_first, at, :] = both[:group]
        nbuf[to_second, at, :] = both[group:]

    for p in range(na):
        near = tile_of(lax.rem(a + p, na), b, c)
        sib_near = tile_of(lax.rem(a + p, na), b, 1 - c)
        far = tile_of(lax.rem(c + p, na), 1 - b, c)
        sib_far = tile_of(lax.rem(1 - c + p, na), 1 - b, 1 - c)
        near_at, far_at = b * 2, (1 - b) * 2
        lag = jnp.where(lax.rem(c + p, na) == a, LAG, 0)
        behind = 0 if p == 0 else 1
        yc, xc = chunks(False, p), chunks(True, p)

        def near_middles(j):
            arrived(p, SIB_NEAR, False, sib_near, j)
            middles(p, j, near, sib_near, near_at + c, near_at + 1 - c)

        def far_middles(j):
            arrived(p, SIB_FAR, False, sib_far, j)
            middles(p, j, far, sib_far, far_at + c, far_at + 1 - c)

        def when_in(i, count, body):
            @pl.when((i >= 0) & (i < count))
            def _():
                body(i)

        if p == 0:
            pcopy.wait()
            qcopy.wait()

            def open_near(j):
                prepare(j)
                near_middles(j)

            loop(AHEAD, open_near)

        def y_step(j):
            if p > 0:
                when_in(j, yc, lambda i: near_forward(p, False, i, start, True))
            when_in(j - behind, yc, lambda i: far_forward(p, False, i, start, True))
            if p == 0:
                when_in(j + AHEAD, yc, open_near)
            else:
                when_in(j - behind - lag, yc, near_middles)
            when_in(j - behind - lag, yc, far_middles)

        loop(yc + behind + LAG, y_step)

        if p == 0:
            @pl.when(z < 2)
            def _():
                pl.semaphore_wait(know_sem.at[0], 1)

            @pl.when(z > 1)
            def _():
                pl.semaphore_wait(know_sem.at[1], 1)

            @pl.when(z == 1)
            def _():
                greet(know_sem.at[2], {"front": front - 1})

            @pl.when(z == 2)
            def _():
                greet(know_sem.at[2], {"front": front + 1})

            @pl.when(jnp.logical_not(inner))
            def _():
                pl.semaphore_wait(know_sem.at[2], 1)

        def process(ch):
            arrived(p, SIB_NEAR, True, sib_near, ch)
            arrived(p, SIB_FAR, True, sib_far, ch)
            at = rows_at(p, ch)
            rows = block // xc
            for item, to in [
                (near, near_at + c), (sib_near, near_at + 1 - c),
                (far, far_at + c), (sib_far, far_at + 1 - c),
            ]:
                xs[to, :rows] = xbuf[item, at, :]

            def schur(d):
                residue = residue_of(d)
                return jnp.dot(
                    xs[residue, :rows], nbuf[residue], preferred_element_type=F32
                ).astype(BF16)

            for d in (2, second, third):
                zbuf[d - 1, p, at] = schur(d)
                zcopy(p, d, ch, z, 3 - d).start()
            recv[z, p, at] = schur(0)

        def x_step(ch):
            if p > 0:
                when_in(ch, xc, lambda i: near_forward(p, True, i, start, True))
            when_in(ch - behind, xc, lambda i: far_forward(p, True, i, start, True))
            if p + 1 < na:
                @pl.when(ch == xc - 1 + behind)
                def _():
                    own_start(p + 1, False)
                    own_start(p + 1, True)
            when_in(ch - behind - lag, xc, process)

        loop(xc + behind + LAG, x_step)

    def wait_send(copy):
        copy.wait_send()

    for is_x in (False, True):
        for p in range(na):
            own_copies(p, is_x, None, wait_send)
            if p > 0:
                near_forward(p, is_x, None, wait_send, False)
            far_forward(p, is_x, None, wait_send, False)

    source = []
    for s in range(4):
        child = 4 * parent + s
        half = half_ref[child, me]
        residue = lax.rem(z - shift_ref[parent, me + n * half] + 4, 4)
        begin = jnp.where(residue // 2 == b, a, lax.rem(residue, 2))
        source.append((
            [lax.rem(q - begin + na, na) for q in range(na)],
            [half * 2 + half_ref[child, 4 * q + residue] for q in range(na)],
        ))

    if na > 1:
        for d in range(1, 4):
            whole(d, na - 1, False).wait_recv()
    last = na - 1
    rows = block // chunks(True, last)

    def assemble(ch):
        for d in range(1, 4):
            zcopy(last, d, ch, lax.rem(z + d, 4), d - 1).wait_recv()

        def strip(i):
            at = pl.ds(pl.multiple_of(ch * rows + i * STRIP, STRIP), STRIP)
            to = pl.ds(pl.multiple_of(i * STRIP, STRIP), STRIP) if staged else at
            target = obuf if staged else out
            for k in range(block // LANES):
                lanes = slice(k * LANES, (k + 1) * LANES)
                held = [
                    [recv[s, p, at, lanes].astype(F32) for p in range(na)] for s in range(4)
                ]
                for q in range(na):
                    picked = []
                    for s, (order, owner) in enumerate(source):
                        tile = held[s][0]
                        for p in range(1, na):
                            tile = jnp.where(order[q] == p, held[s][p], tile)
                        picked.append((tile, owner[q]))
                    for halves in range(4):
                        total = None
                        for tile, own in picked:
                            term = jnp.where(own == halves, tile, 0.0)
                            total = term if total is None else total + term
                        slot = (halves // 2) * (n // 2) + (halves % 2) * na + q
                        target[slot, to, lanes] = total.astype(BF16)

        loop(rows // STRIP, strip)
        if staged:
            copy = pltpu.make_async_copy(obuf, out.at[:, rows_at(last, ch)], out_sem)
            copy.start()
            copy.wait()

    loop(chunks(True, last), assemble)
    for d in range(1, 4):
        whole(d, na, True).wait_send()


def solution(mesh):
    n = mesh.shape["tile"]
    na = n // 4

    def per_device(xb, yb, pb, qb, lr, ur, half, shift):
        block, columns = xb.shape[2:]
        last_rows = block // chunks(True, na - 1)
        most_rows = max(block // count for count in XC)
        anywhere = pl.BlockSpec(memory_space=pl.ANY)
        scalars = [pltpu.SMEM(value.shape, value.dtype) for value in (lr, ur, half, shift)]
        shape = (n, block, block)
        staged = 2 * n * block * block > VMEM_OUT
        out = pl.pallas_call(
            functools.partial(schur_kernel, n, staged),
            out_shape=jax.ShapeDtypeStruct(shape, BF16) if staged else pltpu.VMEM(shape, BF16),
            in_specs=[anywhere] * 8,
            out_specs=anywhere if staged else pl.BlockSpec(memory_space=pltpu.VMEM),
            scratch_shapes=[
                pltpu.VMEM((n, block, columns), BF16),
                pltpu.VMEM((n, block, columns), BF16),
                pltpu.VMEM((block, columns), BF16),
                pltpu.VMEM((block, columns), BF16),
                pltpu.VMEM((columns, block), BF16),
                pltpu.VMEM((columns, block), BF16),
                pltpu.VMEM((4, columns, block), BF16),
                pltpu.VMEM((4, most_rows, columns), BF16),
                pltpu.VMEM((3, na, block, block), BF16),
                pltpu.VMEM((4, na, block, block), BF16),
                pltpu.VMEM((8, columns), F32),
                pltpu.VMEM((n, last_rows, block) if staged else (1, STRIP, block), BF16),
                *scalars,
                pltpu.SemaphoreType.DMA((8,)),
                pltpu.SemaphoreType.DMA((na, 5 + na, 2)),
                pltpu.SemaphoreType.DMA((3, YC[0] + XC[0])),
                pltpu.SemaphoreType.DMA((max(na - 1, 1), 4, YC[1] + XC[1])),
                pltpu.SemaphoreType.DMA((3,)),
                pltpu.SemaphoreType.DMA((3,)),
                pltpu.SemaphoreType.DMA((3, chunks(True, na - 1))),
                pltpu.SemaphoreType.REGULAR((3,)),
                pltpu.SemaphoreType.DMA,
            ],
            compiler_params=pltpu.CompilerParams(
                collective_id=0, has_side_effects=True,
                vmem_limit_bytes=(63 if staged else 56) * 2**20,
            ),
        )(xb, yb, pb, qb, lr, ur, half, shift)
        return out.reshape(1, 1, n * block, block)

    split = P("front", "tile", None, None)
    ranks = P("front", "tile", None)
    return jax.shard_map(
        per_device, mesh=mesh,
        in_specs=(split, split, split, split, ranks, ranks, P(), P()),
        out_specs=split, check_vma=False,
    )
```

time: 136 us -> 128 us (0.941)
  Pallas kernels: 133 us -> 125 us
    pallas_call x1, Pallas kernels: 133 us -> 125 us  [per_device(): pl.pallas_call(functools.partial(schur_kernel, n, staged), out_shape=jax....]
where the time goes in v2:
time: 128 us; the launch traced here: 127 us
  Pallas kernels  125 us (98%)
  local copies, waits for them, and re-layouts  2.02 us (2%)
    pallas_call x1, Pallas kernels, per_device(): pl.pallas_call(functools.partial(schur_kernel, n, staged), out_shape=jax....  125 us

profile of v2, /device:TPU:0, one launch (start us, length us, event | category | flops | bytes accessed | tf_op | source)
XLA Modules:
  0.0 126.6 jit_solution(17933895637700695886)
XLA Ops:
  0.0 124.6 %shard_map.82 = bf16[8,512,512]{2,1,0:T(8,128)(2,1)S(1)} custom-call(bf16[1,1,512,1024]{3,2,1,0:T(8,128)(2,1)} %xb.1, bf16[1,1,512,1024]{3,2,1,0:T(8,128)(2,1)} %yb.1, bf16[1,1,512,1024]{3,2,1,0:T(8,128)(2,1)} %pb.1, bf16[1,1,512,1024]{3,2,1,0:T(8,128)(2,1)} %qb.1, s32[1,1,32]{2,1,0:T(1,128)} %lr_hbm.1, s32[1,1,32]{2,1,0:T(1,128)} %ur_hbm.1, ...), custom_call_target="tpu_custom_call" | custom-call | tf_op jit(solution)/shard_map/pallas_call | solution.py:402
  124.6 2.0 %copy.10 = bf16[1,1,4096,512]{3,2,1,0:T(8,128)(2,1)} copy(bf16[1,1,4096,512]{3,2,1,0:T(8,128)(2,1)S(1)} %bitcast.1) | data formatting | bytes 8388608

commit v3 on v2

--- a/solution.py
+++ b/solution.py
@@ -9,9 +9,12 @@
 
 MESH = pl.DeviceIdType.MESH
 R = 32
-YC = (8, 4)
-XC = (8, 4)
+YC = (8, 8)
+XC = (8, 8)
 LAG = 3
+WINDOW = 4
+PACE = 2
+ZAHEAD = 3
 AHEAD = 3
 STRIP = 16
 LANES = 256
@@ -123,16 +126,27 @@
             do(send(p, 1, FAR, is_x, me, ch, across))
         if p > 0:
             do(send(p, 2, NEAR, is_x, me, ch, peers[p - 1]))
-        else:
-            do(send(p, 0, SIB_NEAR, is_x, me, ch, sib))
 
     def start(copy):
         copy.start()
 
-    def own_start(p, is_x):
-        loop(chunks(is_x, p), lambda ch: own_copies(p, is_x, ch, start))
-
-    own_start(0, False)
+    def when_in(i, count, body):
+        @pl.when((i >= 0) & (i < count))
+        def _():
+            body(i)
+
+    def own_next(p, i):
+        yc, xc = chunks(False, p), chunks(True, p)
+        when_in(i, yc, lambda ch: own_copies(p, False, ch, start))
+        when_in(i - yc, xc, lambda ch: own_copies(p, True, ch, start))
+        if p + 1 < na:
+            when_in(i - yc - xc, WINDOW, lambda ch: own_copies(p + 1, False, ch, start))
+
+    def own_sib(is_x, ch):
+        return send(0, 0, SIB_NEAR, is_x, me, ch, sib)
+
+    loop(WINDOW, lambda ch: own_copies(0, False, ch, start))
+    loop(chunks(False, 0), lambda ch: own_sib(False, ch).start())
 
     @pl.when(inner)
     def _():
@@ -148,7 +162,7 @@
         xbuf[me, at] = (xbuf[me, at].astype(F32) * keep_x).astype(BF16)
 
     loop(chunks(True, 0), open_x)
-    own_start(0, True)
+    loop(chunks(True, 0), lambda ch: own_sib(True, ch).start())
     urcopy.wait()
     halfcopy.wait()
     shiftcopy.wait()
@@ -179,6 +193,14 @@
             send_sem=zsend_sem.at[d - 1], recv_sem=zearly_sem.at[d - 1],
             device_id={"front": parent * 4 + lax.rem(z + d, 4)}, device_id_type=MESH,
         )
+
+    def paced(p, i, every, ahead):
+        ch = i // every + ahead
+
+        @pl.when((i >= 0) & (lax.rem(i, every) == 0) & (ch < chunks(True, p)))
+        def _():
+            for d in (2, second, third):
+                zcopy(p, d, ch, z, 3 - d).start()
 
     def near_forward(p, is_x, ch, do, wait):
         near = tile_of(lax.rem(a + p, na), b, c)
@@ -220,14 +242,12 @@
         nbuf[to_first, at, :] = both[:group]
         nbuf[to_second, at, :] = both[group:]
 
-    for p in range(na):
+    def phase(p):
         near = tile_of(lax.rem(a + p, na), b, c)
         sib_near = tile_of(lax.rem(a + p, na), b, 1 - c)
         far = tile_of(lax.rem(c + p, na), 1 - b, c)
         sib_far = tile_of(lax.rem(1 - c + p, na), 1 - b, 1 - c)
         near_at, far_at = b * 2, (1 - b) * 2
-        lag = jnp.where(lax.rem(c + p, na) == a, LAG, 0)
-        behind = 0 if p == 0 else 1
         yc, xc = chunks(False, p), chunks(True, p)
 
         def near_middles(j):
@@ -237,54 +257,6 @@
         def far_middles(j):
             arrived(p, SIB_FAR, False, sib_far, j)
             middles(p, j, far, sib_far, far_at + c, far_at + 1 - c)
-
-        def when_in(i, count, body):
-            @pl.when((i >= 0) & (i < count))
-            def _():
-                body(i)
-
-        if p == 0:
-            pcopy.wait()
-            qcopy.wait()
-
-            def open_near(j):
-                prepare(j)
-                near_middles(j)
-
-            loop(AHEAD, open_near)
-
-        def y_step(j):
-            if p > 0:
-                when_in(j, yc, lambda i: near_forward(p, False, i, start, True))
-            when_in(j - behind, yc, lambda i: far_forward(p, False, i, start, True))
-            if p == 0:
-                when_in(j + AHEAD, yc, open_near)
-            else:
-                when_in(j - behind - lag, yc, near_middles)
-            when_in(j - behind - lag, yc, far_middles)
-
-        loop(yc + behind + LAG, y_step)
-
-        if p == 0:
-            @pl.when(z < 2)
-            def _():
-                pl.semaphore_wait(know_sem.at[0], 1)
-
-            @pl.when(z > 1)
-            def _():
-                pl.semaphore_wait(know_sem.at[1], 1)
-
-            @pl.when(z == 1)
-            def _():
-                greet(know_sem.at[2], {"front": front - 1})
-
-            @pl.when(z == 2)
-            def _():
-                greet(know_sem.at[2], {"front": front + 1})
-
-            @pl.when(jnp.logical_not(inner))
-            def _():
-                pl.semaphore_wait(know_sem.at[2], 1)
 
         def process(ch):
             arrived(p, SIB_NEAR, True, sib_near, ch)
@@ -305,26 +277,90 @@
 
             for d in (2, second, third):
                 zbuf[d - 1, p, at] = schur(d)
-                zcopy(p, d, ch, z, 3 - d).start()
+                if p == na - 1:
+                    zcopy(p, d, ch, z, 3 - d).start()
+                else:
+                    @pl.when(ch == 0)
+                    def _():
+                        zcopy(p, d, 0, z, 3 - d).start()
             recv[z, p, at] = schur(0)
-
-        def x_step(ch):
+            if p < na - 1:
+                paced(p, ch - 3, 3, 1)
+
+        return near_middles, far_middles, process
+
+    def meet():
+        @pl.when(z < 2)
+        def _():
+            pl.semaphore_wait(know_sem.at[0], 1)
+
+        @pl.when(z > 1)
+        def _():
+            pl.semaphore_wait(know_sem.at[1], 1)
+
+        @pl.when(z == 1)
+        def _():
+            greet(know_sem.at[2], {"front": front - 1})
+
+        @pl.when(z == 2)
+        def _():
+            greet(know_sem.at[2], {"front": front + 1})
+
+        @pl.when(jnp.logical_not(inner))
+        def _():
+            pl.semaphore_wait(know_sem.at[2], 1)
+
+    phases = [phase(p) for p in range(na)]
+    pcopy.wait()
+    qcopy.wait()
+
+    def open_near(j):
+        prepare(j)
+        phases[0][0](j)
+
+    loop(AHEAD, open_near)
+    first_lag = jnp.where(a == c, LAG, 0)
+    bases = [0]
+    for p in range(na):
+        bases.append(bases[-1] + chunks(False, p) + chunks(True, p))
+
+    def everything(e):
+        for p, base in enumerate(bases[:-1]):
+            yc, xc = chunks(False, p), chunks(True, p)
+            behind = 0 if p == 0 else 1
+
+            def both(forward, i):
+                when_in(i, yc, lambda j: forward(p, False, j, start, True))
+                when_in(i - yc, xc, lambda ch: forward(p, True, ch, start, True))
+
             if p > 0:
-                when_in(ch, xc, lambda i: near_forward(p, True, i, start, True))
-            when_in(ch - behind, xc, lambda i: far_forward(p, True, i, start, True))
-            if p + 1 < na:
-                @pl.when(ch == xc - 1 + behind)
+                both(near_forward, e - base)
+            both(far_forward, e - base - behind)
+            when_in(e - base, yc + xc, lambda i: own_next(p, i + WINDOW))
+            if p > 0:
+                when_in(e - base, yc + xc, lambda i: paced(p - 1, i, PACE, ZAHEAD))
+        for p, base in enumerate(bases[:-1]):
+            yc, xc = chunks(False, p), chunks(True, p)
+            near_middles, far_middles, process = phases[p]
+            if p == 0:
+                when_in(e + AHEAD, yc, open_near)
+            work = e - base - (first_lag if p == 0 else LAG + 1)
+            if p > 0:
+                when_in(work, yc, near_middles)
+            when_in(work, yc, far_middles)
+            if p == 0:
+                @pl.when(work == yc)
                 def _():
-                    own_start(p + 1, False)
-                    own_start(p + 1, True)
-            when_in(ch - behind - lag, xc, process)
-
-        loop(xc + behind + LAG, x_step)
+                    meet()
+            when_in(work - yc, xc, process)
+
+    loop(bases[-1] + LAG + 1, everything)
 
     def wait_send(copy):
         copy.wait_send()
 
     for is_x in (False, True):
+        own_sib(is_x, None).wait_send()
         for p in range(na):
             own_copies(p, is_x, None, wait_send)
             if p > 0:

time: 128 us -> 121 us (0.945); the launches traced: 127 us -> 121 us
  Pallas kernels: 125 us -> 119 us
    pallas_call x1, Pallas kernels: 125 us -> 119 us  [per_device(): pl.pallas_call(functools.partial(schur_kernel, n, staged), out_shape=jax....]
where the time goes in v3:
time: 121 us
  Pallas kernels  119 us (98%)
  local copies, waits for them, and re-layouts  2.02 us (2%)
    pallas_call x1, Pallas kernels, per_device(): pl.pallas_call(functools.partial(schur_kernel, n, staged), out_shape=jax....  119 us

profile of v3, /device:TPU:0, one launch (start us, length us, event | category | flops | bytes accessed | tf_op | source)
XLA Modules:
  0.0 121.1 jit_solution(2753415249767990310)
XLA Ops:
  0.0 119.1 %shard_map.82 = bf16[8,512,512]{2,1,0:T(8,128)(2,1)S(1)} custom-call(bf16[1,1,512,1024]{3,2,1,0:T(8,128)(2,1)} %xb.1, bf16[1,1,512,1024]{3,2,1,0:T(8,128)(2,1)} %yb.1, bf16[1,1,512,1024]{3,2,1,0:T(8,128)(2,1)} %pb.1, bf16[1,1,512,1024]{3,2,1,0:T(8,128)(2,1)} %qb.1, s32[1,1,32]{2,1,0:T(1,128)} %lr_hbm.1, s32[1,1,32]{2,1,0:T(1,128)} %ur_hbm.1, ...), custom_call_target="tpu_custom_call" | custom-call | tf_op jit(solution)/shard_map/pallas_call | solution.py:438
  119.1 2.0 %copy.10 = bf16[1,1,4096,512]{3,2,1,0:T(8,128)(2,1)} copy(bf16[1,1,4096,512]{3,2,1,0:T(8,128)(2,1)S(1)} %bitcast.1) | data formatting | bytes 8388608

commit v4 on v3

--- a/solution.py
+++ b/solution.py
@@ -344,7 +344,7 @@
             near_middles, far_middles, process = phases[p]
             if p == 0:
                 when_in(e + AHEAD, yc, open_near)
-            work = e - base - (first_lag if p == 0 else LAG + 1)
+            work = e - base - (first_lag if p == 0 else LAG)
             if p > 0:
                 when_in(work, yc, near_middles)
             when_in(work, yc, far_middles)

time: 121 us -> 121 us (level)
  no operation moved by 1% of the time
where the time goes in v4:
time: 121 us
  Pallas kernels  119 us (98%)
  local copies, waits for them, and re-layouts  2.02 us (2%)
    pallas_call x1, Pallas kernels, per_device(): pl.pallas_call(functools.partial(schur_kernel, n, staged), out_shape=jax....  119 us

profile of v4, /device:TPU:0, one launch (start us, length us, event | category | flops | bytes accessed | tf_op | source)
XLA Modules:
  0.0 121.2 jit_solution(13050065562582078230)
XLA Ops:
  0.0 119.1 %shard_map.82 = bf16[8,512,512]{2,1,0:T(8,128)(2,1)S(1)} custom-call(bf16[1,1,512,1024]{3,2,1,0:T(8,128)(2,1)} %xb.1, bf16[1,1,512,1024]{3,2,1,0:T(8,128)(2,1)} %yb.1, bf16[1,1,512,1024]{3,2,1,0:T(8,128)(2,1)} %pb.1, bf16[1,1,512,1024]{3,2,1,0:T(8,128)(2,1)} %qb.1, s32[1,1,32]{2,1,0:T(1,128)} %lr_hbm.1, s32[1,1,32]{2,1,0:T(1,128)} %ur_hbm.1, ...), custom_call_target="tpu_custom_call" | custom-call | tf_op jit(solution)/shard_map/pallas_call | solution.py:438
  119.1 2.0 %copy.10 = bf16[1,1,4096,512]{3,2,1,0:T(8,128)(2,1)} copy(bf16[1,1,4096,512]{3,2,1,0:T(8,128)(2,1)S(1)} %bitcast.1) | data formatting | bytes 8388608
